TPU v7x, 32 devices: a whole 2x2x4 slice. The times are simulated.
32 devices in a mesh: pole: 2 (over y), prow: 4 (over z), pcol: 4 (over x, core).
Axes of the slice: x: 2, y: 2, z: 4, core: 2. Of those that a mesh axis runs over, the one named last changes fastest.
Arguments:
- ainv_anc: bfloat16 [2, 4096, 2048], P(None, ('pole', 'prow'), 'pcol'), parts along dimension 1, may hold values from -6 to 6
- panel: bfloat16 [2, 8, 1024, 256], P(None, 'pole', ('pcol', 'prow')), parts along dimension 1, may hold values from -6 to 6
- u_inv: bfloat16 [2, 8, 256, 256], P(None, 'pole'), parts along dimension 1, may hold values from -0.01171875 to 0.01171875
- k_inv: float32 [2, 8, 256, 256], P(None, ('pole', 'pcol')), parts along dimension 1, may hold values from -6 to 6
- structure: int32 [4, 4], replicated, may hold values from -1 to 7, as said below
Outputs:
- sel_inv: float32 [2, 4096, 1024], P(None, ('pole', 'prow'), 'pcol'), parts along dimension 1
- diag_inv: float32 [2, 8, 256, 256], P(None, ('pole', 'pcol')), parts along dimension 1
There are 2 independent parts, one for each index of `pole`. A program takes and returns all parts, laid end to end along the dimension named above; an argument that names none is the same for every part. Nothing has to cross between parts.
Inputs may be any that keep to these rules, and one draw needn't show every extreme that they name: `structure`: slots g * 1 to (g + 1) * 1 - 1 of row k hold distinct blocks of g * 2 to (g + 1) * 2 - 1 in rising order, followed by -1 for empty slots; each such group of each row holds at least one block, and for every g some row fills all 1 slots of group g.
All inputs are finite; a program needn't handle non-finite values.
Results may differ from a plain program's by a relative error of at most 0.005.
Values may be sent and summed in bfloat16 or wider, within the bound.
A program may use at most 128 MiB of HBM per device.

v0:
```python
import jax
import jax.numpy as jnp
from jax import lax
from jax.sharding import PartitionSpec as P


def complex_quad(z_part, s_part):
    highest = lax.Precision.HIGHEST

    def single(left, right):
        return jnp.einsum("kra,rkb->kab", left, right, precision=highest)

    real = single(z_part[0], s_part[0]) - single(z_part[1], s_part[1])
    imag = single(z_part[0], s_part[1]) + single(z_part[1], s_part[0])
    return jnp.stack([real, imag])


def local(ainv_anc, panel, u_inv, k_inv, structure):
    block_width = u_inv.shape[-1]
    total_k = u_inv.shape[1]
    own_k = k_inv.shape[1]
    n_cols = lax.axis_size("pcol")
    row_here = lax.axis_index("prow")
    col_here = lax.axis_index("pcol")
    row_blocks = ainv_anc.shape[1] // block_width
    group_blocks = ainv_anc.shape[2] // block_width
    group_slots = structure.shape[1] // n_cols
    rows_all = row_blocks * block_width
    col_struct = lax.dynamic_slice_in_dim(structure, col_here * group_slots, group_slots, 1)
    slot_live = col_struct >= 0
    slot_pos = col_struct - col_here * group_blocks
    first_block = row_here * row_blocks
    target = first_block + jnp.arange(row_blocks, dtype=jnp.int32)
    rows_in = lax.all_gather(panel, "prow", axis=2, tiled=True)

    def single(left, right):
        return jnp.einsum("knb,kbc->knc", left, right, preferred_element_type=jnp.float32)

    real = single(rows_in[0], u_inv[0]) - single(rows_in[1], u_inv[1])
    imag = single(rows_in[0], u_inv[1]) + single(rows_in[1], u_inv[0])
    placed = jnp.stack([real, imag]).astype(jnp.bfloat16)
    placed = placed.reshape(2, total_k, group_slots, block_width, block_width)
    placed = jnp.where(slot_live[None, :, :, None, None], placed, jnp.zeros((), jnp.bfloat16))
    block_ids = jnp.arange(group_blocks, dtype=jnp.int32)
    pick_table = (slot_pos[:, :, None] == block_ids[None, None, :]).astype(jnp.bfloat16)
    ainv_blocks = ainv_anc.reshape(2, rows_all, group_blocks, block_width)

    def one_node(items):
        table_k, rows_k = items
        picked = jnp.einsum(
            "sg,cigw->cisw", table_k, ainv_blocks, preferred_element_type=jnp.float32
        )
        picked = picked.astype(jnp.bfloat16).reshape(2, rows_all, group_slots * block_width)
        right = rows_k.reshape(2, group_slots * block_width, block_width)
        real = jnp.dot(picked[0], right[0], preferred_element_type=jnp.float32) - jnp.dot(
            picked[1], right[1], preferred_element_type=jnp.float32
        )
        imag = jnp.dot(picked[0], right[1], preferred_element_type=jnp.float32) + jnp.dot(
            picked[1], right[0], preferred_element_type=jnp.float32
        )
        return jnp.stack([real, imag])

    per_node = lax.map(one_node, (pick_table, jnp.moveaxis(placed, 1, 0)))
    partial_value = jnp.transpose(per_node, (1, 2, 0, 3))
    row_table = (col_struct[:, None, :] == target[None, :, None]).astype(jnp.bfloat16)
    z_rows = jnp.einsum("kts,ckswb->cktwb", row_table, placed, preferred_element_type=jnp.float32)
    z_rows = z_rows.astype(jnp.bfloat16).reshape(2, total_k, rows_all, block_width)
    summed = lax.psum_scatter(
        partial_value.reshape(2, rows_all, total_k * block_width),
        "pcol",
        scatter_dimension=2,
        tiled=True,
    )
    own_struct = lax.dynamic_slice_in_dim(structure, col_here * own_k, own_k, 0)
    member = jnp.any(own_struct[:, :, None] == target[None, None, :], axis=1)
    selected = -summed.reshape(2, row_blocks, block_width, own_k, block_width)
    selected = jnp.where(member.T[None, :, None, :, None], selected, 0.0)
    sel_inv = selected.reshape(2, rows_all, own_k * block_width)
    received = lax.all_to_all(z_rows, "pcol", split_axis=1, concat_axis=1, tiled=True)
    z_own = (
        received.astype(jnp.float32).reshape(2, n_cols, own_k, rows_all, block_width).sum(axis=1)
    )
    quad_term = complex_quad(z_own, selected.reshape(2, rows_all, own_k, block_width))
    total_sum = lax.psum(quad_term, "prow")
    diag_inv = k_inv - total_sum
    return (sel_inv, diag_inv)


def solution(mesh):
    placed = (
        P(None, ("pole", "prow"), "pcol"),
        P(None, "pole", ("pcol", "prow"), None),
        P(None, "pole", None, None),
        P(None, ("pole", "pcol"), None, None),
        P(),
    )
    return jax.shard_map(
        local,
        mesh=mesh,
        in_specs=placed,
        out_specs=(P(None, ("pole", "prow"), "pcol"), P(None, ("pole", "pcol"), None, None)),
        check_vma=False,
    )
```

profile of v0, /device:TPU:0, one launch (start us, length us, event | category | flops | bytes accessed | tf_op | source)
XLA Modules:
  0.0 170.8 jit_solution(10218093751577018464)
XLA Ops:
  7.2 0.7 all-gather.2.cloned.1.call-update
  7.9 0.0 reduce-scatter.2.cloned.1.call-start
  8.0 1.3 reshape.276
  9.3 0.9 compare_reduce_fusion
  10.2 0.9 dynamic-slice_reduce_fusion
  11.1 0.1 compare_convert_fusion
  11.2 29.1 %all-gather.2.cloned.1.call-done = bf16[2,4,256,256]{3,2,1,0:T(8,128)(2,1)} async-done(((bf16[2,4,64,256]{3,2,1,0:T(8,128)(2,1)}), bf16[2,4,256,256]{3,2,1,0:T(8,128)(2,1)}) %all-gather.2.cloned.1.call-update) | async-done | bytes 1048592 | tf_op jit(solution)/shard_map/all_gather | solution.py:34
  40.3 1.6 fusion.13
  41.9 1.3 fusion.17
  43.3 0.3 fusion.9
  43.6 0.3 fusion.8
  43.9 0.2 fusion.12
  44.1 13.4 %while.10 = (s32[]{:T(128)}, f32[4,2,512,256]{3,2,1,0:T(8,128)}, bf16[4,1,2]{2,1,0:T(2,128)(2,1)S(1)}, bf16[2,512,2,256]{3,2,1,0:T(2,128)(2,1)S(1)}, bf16[4,2,1,256,256]{4,3,0,2,1:T(8,128)(2,1)S(1)}, /*index=5*/s32[]{:T(128)}) while((s32[]{:T(128)}, f32[4,2,512,256]{3,2,1,0:T(8,128)}, bf16[4,1,2]{2,1,0:T(2,128)(2,1)S(1)}, ...), condition=%wide.region_2.3_spmd, body=%wide.region_1.2_spmd.sunk | while | flops 270008320 | bytes 9962073 | solution.py:63
  44.1 1.2 fusion.42
  45.3 0.1 copy.25
  45.4 0.2 fusion.45
  45.7 0.2 fusion.46
  45.9 0.2 fusion.43
  46.1 0.2 fusion.44
  46.4 1.0 fusion.47
  47.4 1.2 fusion.42
  48.7 0.1 copy.25
  48.8 0.2 fusion.45
  49.0 0.2 fusion.46
  49.2 0.2 fusion.43
  49.5 0.2 fusion.44
  49.7 1.1 fusion.47
  50.8 1.2 fusion.42
  52.0 0.1 copy.25
  52.1 0.2 fusion.45
  52.4 0.2 fusion.46
  52.6 0.2 fusion.43
  52.8 0.2 fusion.44
  53.1 1.1 fusion.47
  54.2 1.2 fusion.42
  55.4 0.1 copy.25
  55.5 0.2 fusion.45
  55.7 0.2 fusion.46
  56.0 0.2 fusion.43
  56.2 0.2 fusion.44
  56.4 1.0 fusion.47
  57.5 4.8 %copy.21 = f32[4,2,64,8,256]{4,3,0,2,1:T(8,128)} copy(f32[4,2,64,8,256]{4,3,2,1,0:T(8,128)} %bitcast.135) | data formatting | bytes 8388608 | tf_op jit(solution)/shard_map/reshape | solution.py:69
  62.3 0.1 compare_convert_fusion.1
  62.3 0.2 convert_bitcast_fusion
  62.5 0.5 multiply_convert_fusion
  63.0 1.5 copy.17
  64.5 3.8 %all-to-all-start = ((bf16[2,4,512,256]{3,2,0,1:T(8,128)(2,1)}), bf16[2,4,512,256]{3,2,0,1:T(8,128)(2,1)S(1)}, u32[]{:S(2)}, u32[]{:S(2)}) async-start(bf16[2,4,512,256]{3,2,0,1:T(8,128)(2,1)} %copy.17), calls=%async_computation.1 | async-start | bytes 4194304 | tf_op jit(solution)/shard_map/all_to_all | solution.py:79
  68.2 0.0 all-reduce.2.cloned.1.call-start
  68.3 0.7 dynamic-slice_bitcast_fusion.1
  69.0 0.1 compare_reduce_fusion.1
  69.1 0.1 broadcast_in_dim.52
  69.2 36.9 %all-to-all-done = bf16[2,4,512,256]{3,2,0,1:T(8,128)(2,1)S(1)} async-done(((bf16[2,4,512,256]{3,2,0,1:T(8,128)(2,1)}), bf16[2,4,512,256]{3,2,0,1:T(8,128)(2,1)S(1)}, u32[]{:S(2)}, u32[]{:S(2)}) %all-to-all-start) | async-done | bytes 2097184 | tf_op jit(solution)/shard_map/all_to_all | solution.py:79
  106.1 0.3 convert_reduce_fusion
  106.4 11.5 %reduce-scatter.2.cloned.1.call-done = f32[2,512,256]{2,1,0:T(8,128)} async-done(((f32[2,512,1024]{2,1,0:T(8,128)}), f32[2,512,256]{2,1,0:T(8,128)}) %reduce-scatter.2.cloned.1.call-update) | async-done | bytes 1048592 | tf_op jit(solution)/shard_map/reduce_scatter | solution.py:68
  117.9 2.3 %fusion.26 = (f32[2,512,256]{2,1,0:T(8,128)S(1)}, f32[2,512,256]{2,1,0:T(8,128)}) fusion(f32[2,512,256]{2,1,0:T(8,128)} %reduce-scatter.2.cloned.1.call-done, pred[512]{0:T(512)(128)(4,1)S(1)} %broadcast_in_dim.53), kind=kLoop, calls=%fused_computation.59 | loop fusion | flops 524288 | bytes 3146240 | tf_op jit(solution)/shard_map/neg | solution.py:76
  120.2 0.1 broadcast_select_fusion
  120.4 0.1 fusion.25
  120.5 1.0 fusion.19
  121.5 1.0 fusion.20
  122.5 1.0 fusion.10
  123.5 1.0 fusion.11
  124.5 0.8 pad_maximum_fusion
  125.4 37.0 %all-reduce.2.cloned.1.call-done = f32[2,1,256,256]{3,2,1,0:T(8,128)} async-done(((f32[2,1,256,256]{3,2,1,0:T(8,128)}), f32[2,1,256,256]{3,2,1,0:T(8,128)}) %all-reduce.2.cloned.1.call-update) | async-done | bytes 524304 | tf_op jit(solution)/shard_map/psum | solution.py:84
  162.4 1.9 %sub.26 = f32[2,1,256,256]{3,2,1,0:T(8,128)} subtract(f32[2,1,256,256]{3,2,1,0:T(8,128)S(1)} %copy-done.2, f32[2,1,256,256]{3,2,1,0:T(8,128)} %all-reduce.2.cloned.1.call-done) | non-fusion elementwise | flops 131072 | bytes 1572864 | tf_op jit(solution)/shard_map/sub | solution.py:85
  (16 shorter events, 0.2 us)
Async XLA Ops:
  7.2 34.7 %copy-start = (bf16[2,4,256,256]{3,2,1,0:T(8,128)(2,1)S(1)}, bf16[2,4,256,256]{3,2,1,0:T(8,128)(2,1)}, u32[]{:S(2)}) copy-start(bf16[2,4,256,256]{3,2,1,0:T(8,128)(2,1)} %param.9) | copy-start | bytes 3145732
  7.2 33.1 %all-gather.2.cloned.1.call-start = ((), (), s32[]{:S(2)}) async-start(), calls=%async_computation.2 | async-start | bytes 1310720 | tf_op jit(solution)/shard_map/all_gather | solution.py:34
  7.9 110.0 %reduce-scatter.2.cloned.1.call-start = ((), (), s32[]{:S(2)}) async-start(), calls=%async_computation.3 | async-start | bytes 5242880 | tf_op jit(solution)/shard_map/reduce_scatter | solution.py:68
  40.3 3.0 %copy-start.1 = (bf16[2,4,256,256]{3,2,1,0:T(8,128)(2,1)S(1)}, bf16[2,4,256,256]{3,2,1,0:T(8,128)(2,1)}, u32[]{:S(2)}) copy-start(bf16[2,4,256,256]{3,2,1,0:T(8,128)(2,1)} %all-gather.2.cloned.1.call-done) | copy-start | bytes 3145732
  64.5 41.6 %all-to-all-start = ((bf16[2,4,512,256]{3,2,0,1:T(8,128)(2,1)}), bf16[2,4,512,256]{3,2,0,1:T(8,128)(2,1)S(1)}, u32[]{:S(2)}, u32[]{:S(2)}) async-start(bf16[2,4,512,256]{3,2,0,1:T(8,128)(2,1)} %copy.17), calls=%async_computation.1 | async-start | bytes 4194304 | tf_op jit(solution)/shard_map/all_to_all | solution.py:79
  68.2 94.1 %all-reduce.2.cloned.1.call-start = ((), (), s32[]{:S(2)}) async-start(), calls=%async_computation.4 | async-start | bytes 1048576 | tf_op jit(solution)/shard_map/psum | solution.py:84
  120.4 41.9 %copy-start.2 = (f32[2,1,256,256]{3,2,1,0:T(8,128)S(1)}, f32[2,1,256,256]{3,2,1,0:T(8,128)}, u32[]{:S(2)}) copy-start(f32[2,1,256,256]{3,2,1,0:T(8,128)} %param.10) | copy-start | bytes 1572868
Sparse Core Ops, SparseCore 0:
  9.6 30.6 all-gather.1
  62.4 55.4 reduce-scatter.1
  125.5 36.8 all-reduce.1
where the time goes:
time: 171 us
  waiting for transfers between devices  115 us (67%)
  matrix products  16.1 us (9%)
  between operations  13.9 us (8%)
  other arithmetic  12.6 us (7%)
  local copies, waits for them, and re-layouts  8.88 us (5%)
  starting transfers between devices  3.88 us (2%)
    psum x1, waiting for transfers between devices, local(): total_sum = lax.psum(quad_term, 'prow')  37 us
    all_to_all x1, waiting for transfers between devices, local(): lax.all_to_all(z_rows, 'pcol', split_axis=1, concat_axis=1, tiled=True)  36.9 us
    all_gather x1, waiting for transfers between devices, local(): rows_in = lax.all_gather(panel, 'prow', axis=2, tiled=True)  29.1 us
    reduce_scatter x1, waiting for transfers between devices, local(): lax.psum_scatter(partial_value.reshape(2, rows_all, total_k * block_width...  11.5 us
    dot_general x4, matrix products, one_node(): jnp.einsum('sg,cigw->cisw', table_k, ainv_blocks, preferred_element_type=...  4.94 us
    reshape x1, local copies, waits for them, and re-layouts, local(): partial_value.reshape(2, rows_all, total_k * block_width)  4.76 us
    dynamic_update_slice x4, other arithmetic, local(): per_node = lax.map(one_node, (pick_table, jnp.moveaxis(placed, 1, 0)))  4.27 us
    dot_general x4, matrix products, single(): return jnp.einsum('kra,rkb->kab', left, right, precision=highest)  4.02 us
  transfers between devices with their start and end apart: 4, of which 4 were waited for; matrix products, arithmetic and copies ran while one was open for 4% of the time, Pallas kernels for 0%

commit v1 on v0

--- a/solution.py
+++ b/solution.py
@@ -1,7 +1,274 @@
+import functools
+
 import jax
 import jax.numpy as jnp
 from jax import lax
+from jax.experimental import pallas as pl
+from jax.experimental.pallas import tpu as pltpu
 from jax.sharding import PartitionSpec as P
+
+BF16 = jnp.bfloat16
+F32 = jnp.float32
+
+
+def cdot(left, right, dims=(((1,), (0,)), ((), ()))):
+    def single(x, y):
+        return lax.dot_general(x, y, dims, preferred_element_type=F32)
+
+    real = single(left[0], right[0]) - single(left[1], right[1])
+    imag = single(left[0], right[1]) + single(left[1], right[0])
+    return real, imag
+
+
+def remote(src, dst, send_sem, recv_sem, where):
+    return pltpu.make_async_remote_copy(
+        src_ref=src,
+        dst_ref=dst,
+        send_sem=send_sem,
+        recv_sem=recv_sem,
+        device_id=where,
+        device_id_type=pl.DeviceIdType.MESH,
+    )
+
+
+def kernel(
+    n_rows, n_cols, table, a_hbm, panel_hbm, u_hbm, r_out, t_out,
+    av, pv, uv, pr, gather, pick_out, pick_in, acc, qsend_buf, qrecv_buf, tot,
+    local_sem, p_send, p_recv, a_send, a_recv, g_send, g_recv, q_send, q_recv, t_send, t_recv,
+):
+    row = lax.axis_index("prow")
+    col = lax.axis_index("pcol")
+    width = u_hbm.shape[-1]
+    part = panel_hbm.shape[2]
+    pairs = n_cols // 2
+    row_blocks = a_hbm.shape[1] // width
+    col_blocks = a_hbm.shape[2] // width
+
+    def peer(unit):
+        return ((col // 2 + unit // 2) % pairs) * 2 + (col + unit) % 2
+
+    copy_p = pltpu.make_async_copy(panel_hbm, pv, local_sem.at[0])
+    copy_u = pltpu.make_async_copy(u_hbm.at[:, col], uv, local_sem.at[1])
+    copy_a = pltpu.make_async_copy(a_hbm, av, local_sem.at[2])
+    copy_p.start()
+    copy_u.start()
+    copy_a.start()
+
+    barrier = pltpu.get_barrier_semaphore()
+    for unit in range(1, n_cols):
+        pl.semaphore_signal(barrier, inc=1, device_id={"pcol": peer(unit)}, device_id_type=pl.DeviceIdType.MESH)
+    for step in range(1, n_rows):
+        pl.semaphore_signal(
+            barrier, inc=1, device_id={"prow": (row + step) % n_rows}, device_id_type=pl.DeviceIdType.MESH
+        )
+    pl.semaphore_wait(barrier, n_cols + n_rows - 2)
+
+    def panel_copy(unit, source):
+        return remote(
+            pv.at[:, peer(unit)], pr.at[source], p_send.at[unit], p_recv.at[source], {"pcol": peer(unit)}
+        )
+
+    def pick_copy(unit, source):
+        return remote(
+            pick_out.at[unit], pick_in.at[source], a_send.at[unit], a_recv.at[source], {"pcol": peer(unit)}
+        )
+
+    def line_copy(unit, chunk, step, side):
+        block = gather.at[unit, :, chunk]
+        there = row + 1 if side == 0 else row - 1
+        return remote(block, block, g_send.at[unit, side, step], g_recv.at[unit, chunk], {"prow": there})
+
+    copy_p.wait()
+    for unit in range(1, n_cols):
+        panel_copy(unit, col).start()
+    copy_u.wait()
+
+    def scale(unit):
+        slot = peer(unit)
+        if unit == 0:
+            left = (pv[0, col], pv[1, col])
+        else:
+            panel_copy(unit, slot).wait_recv()
+            left = (pr[slot, 0], pr[slot, 1])
+        real, imag = cdot(left, (uv[0], uv[1]))
+        live = (jnp.full((1, width), table[col, slot]) >= 0).astype(F32)
+        gather[unit, 0, row] = (real * live).astype(BF16)
+        gather[unit, 1, row] = (imag * live).astype(BF16)
+
+        @pl.when(row < n_rows - 1)
+        def _():
+            line_copy(unit, row, 0, 0).start()
+
+        @pl.when(row > 0)
+        def _():
+            line_copy(unit, row, 0, 1).start()
+
+    def pick(unit):
+        node = peer(unit)
+        top = jnp.full((1, width), table[node, row]) - row * row_blocks
+        side = jnp.full((1, width), table[node, col]) - col * col_blocks
+        for plane in range(2):
+            total = None
+            for i in range(row_blocks):
+                for j in range(col_blocks):
+                    keep = ((top == i) & (side == j)).astype(F32).astype(BF16)
+                    block = av[plane, i * width : (i + 1) * width, j * width : (j + 1) * width] * keep
+                    total = block if total is None else total + block
+            pick_out[unit, plane] = total
+
+    scale(0)
+    scale(1)
+    copy_a.wait()
+    order = list(range(2, n_cols)) + [1]
+    for unit in order:
+        pick(unit)
+        pick_copy(unit, col).start()
+    pick(0)
+    for unit in range(2, n_cols):
+        scale(unit)
+
+    for unit in range(n_cols):
+        for step in range(1, n_rows):
+            below, above = row - step, row + step
+
+            @pl.when(below >= 0)
+            def _():
+                line_copy(unit, below, step, 0).wait_recv()
+
+                @pl.when(row < n_rows - 1)
+                def _():
+                    line_copy(unit, below, step, 0).start()
+
+            @pl.when(above <= n_rows - 1)
+            def _():
+                line_copy(unit, above, step, 1).wait_recv()
+
+                @pl.when(row > 0)
+                def _():
+                    line_copy(unit, above, step, 1).start()
+
+        slot = peer(unit)
+        if unit == 0:
+            left = (pick_out[0, 0], pick_out[0, 1])
+        else:
+            pick_copy(unit, slot).wait_recv()
+            left = (pick_in[slot, 0], pick_in[slot, 1])
+        right = tuple(gather[unit, plane].reshape(width, width) for plane in range(2))
+        real, imag = cdot(left, right)
+        if unit == 0:
+            acc[0] = real
+            acc[1] = imag
+        else:
+            acc[0] += real
+            acc[1] += imag
+
+    live = (jnp.full((1, width), table[col, row]) >= 0).astype(F32)
+    unit_here = ((row // 2 - col // 2 + pairs) % pairs) * 2 + (row + col) % 2
+    z = tuple(gather[unit_here, plane].reshape(width, width) for plane in range(2))
+    r = (acc[0] * live, acc[1] * live)
+    r_out[0] = r[0]
+    r_out[1] = r[1]
+    real, imag = cdot(z, (r[0].astype(BF16), r[1].astype(BF16)), (((0,), (0,)), ((), ())))
+    acc[0] = real
+    acc[1] = imag
+    for plane in range(2):
+        qsend_buf[:, plane] = acc[plane].reshape(n_rows, part, width).astype(BF16)
+
+    def quad_copy(step, source):
+        there = (row + step) % n_rows
+        return remote(qsend_buf.at[there], qrecv_buf.at[source], q_send.at[step], q_recv.at[source], {"prow": there})
+
+    def total_copy(step, source):
+        there = (row + step) % n_rows
+        return remote(tot.at[source], tot.at[source], t_send.at[step], t_recv.at[source], {"prow": there})
+
+    for step in range(1, n_rows):
+        quad_copy(step, row).start()
+    mine = pl.ds(pl.multiple_of(row * part, part), part)
+    sums = [acc[0, mine, :], acc[1, mine, :]]
+    for step in range(1, n_rows):
+        source = (row + step) % n_rows
+        quad_copy(step, source).wait_recv()
+        for plane in range(2):
+            sums[plane] = sums[plane] + qrecv_buf[source, plane].astype(F32)
+    for plane in range(2):
+        tot[row, plane] = sums[plane].astype(BF16)
+    for step in range(1, n_rows):
+        total_copy(step, row).start()
+    for step in range(1, n_rows):
+        total_copy(step, (row + step) % n_rows).wait_recv()
+    for plane in range(2):
+        t_out[plane] = tot[:, plane].reshape(width, width)
+
+    for unit in range(1, n_cols):
+        panel_copy(unit, col).wait_send()
+        pick_copy(unit, col).wait_send()
+    for unit in range(n_cols):
+        for step in range(n_rows):
+            below, above = row - step, row + step
+
+            @pl.when((below >= 0) & (row < n_rows - 1))
+            def _():
+                line_copy(unit, below, step, 0).wait_send()
+
+            @pl.when((above <= n_rows - 1) & (row > 0))
+            def _():
+                line_copy(unit, above, step, 1).wait_send()
+
+    for step in range(1, n_rows):
+        quad_copy(step, row).wait_send()
+        total_copy(step, row).wait_send()
+
+
+def compact(ainv_anc, panel, u_inv, k_inv, structure):
+    n_rows, n_cols = lax.axis_size("prow"), lax.axis_size("pcol")
+    width, part = u_inv.shape[-1], panel.shape[2]
+    row_blocks = ainv_anc.shape[1] // width
+    hbm = pl.BlockSpec(memory_space=pl.ANY)
+    vmem = pl.BlockSpec(memory_space=pltpu.VMEM)
+    dma = pltpu.SemaphoreType.DMA
+    r, total = pl.pallas_call(
+        functools.partial(kernel, n_rows, n_cols),
+        out_shape=(
+            jax.ShapeDtypeStruct((2, width, width), F32),
+            jax.ShapeDtypeStruct((2, width, width), BF16),
+        ),
+        in_specs=[pl.BlockSpec(memory_space=pltpu.SMEM), hbm, hbm, hbm],
+        out_specs=(vmem, vmem),
+        scratch_shapes=[
+            pltpu.VMEM(ainv_anc.shape, BF16),
+            pltpu.VMEM(panel.shape, BF16),
+            pltpu.VMEM((2, width, width), BF16),
+            pltpu.VMEM((n_cols, 2, part, width), BF16),
+            pltpu.VMEM((n_cols, 2, n_rows, part, width), BF16),
+            pltpu.VMEM((n_cols, 2, width, width), BF16),
+            pltpu.VMEM((n_cols, 2, width, width), BF16),
+            pltpu.VMEM((2, width, width), F32),
+            pltpu.VMEM((n_rows, 2, part, width), BF16),
+            pltpu.VMEM((n_rows, 2, part, width), BF16),
+            pltpu.VMEM((n_rows, 2, part, width), BF16),
+            dma((3,)),
+            dma((n_cols,)),
+            dma((n_cols,)),
+            dma((n_cols,)),
+            dma((n_cols,)),
+            dma((n_cols, 2, n_rows)),
+            dma((n_cols, n_rows)),
+            dma((n_rows,)),
+            dma((n_rows,)),
+            dma((n_rows,)),
+            dma((n_rows,)),
+        ],
+        compiler_params=pltpu.CompilerParams(
+            collective_id=0, has_side_effects=True, vmem_limit_bytes=24 * 1024 * 1024
+        ),
+    )(structure, ainv_anc, panel, u_inv)
+    row, col = lax.axis_index("prow"), lax.axis_index("pcol")
+    named = structure[col, row] - row * row_blocks
+    keep = named == jnp.arange(row_blocks, dtype=jnp.int32)
+    sel_inv = jnp.where(keep[None, :, None, None], -r[:, None], 0.0)
+    diag_inv = k_inv + total[:, None].astype(F32)
+    return sel_inv.reshape(2, row_blocks * width, width), diag_inv
 
 
 def complex_quad(z_part, s_part):
@@ -17,6 +284,15 @@
 
 def local(ainv_anc, panel, u_inv, k_inv, structure):
     block_width = u_inv.shape[-1]
+    cols = lax.axis_size("pcol")
+    if (
+        structure.shape[1] == cols
+        and lax.axis_size("prow") == cols
+        and ainv_anc.shape[1] == ainv_anc.shape[2]
+        and u_inv.shape[1] == cols
+        and cols % 2 == 0
+    ):
+        return compact(ainv_anc, panel, u_inv, k_inv, structure)
     total_k = u_inv.shape[1]
     own_k = k_inv.shape[1]
     n_cols = lax.axis_size("pcol")

time: 171 us -> 51.8 us (0.30)
  waiting for transfers between devices: 115 us -> 0 us
  Pallas kernels: 0 us -> 43.4 us
  matrix products: 16.1 us -> 0 us
  between operations: 13.9 us -> 1.33 us
  other arithmetic: 12.6 us -> 2.02 us
  local copies, waits for them, and re-layouts: 8.88 us -> 4.75 us
  starting transfers between devices: 3.88 us -> 0 us
    pallas_call x0 -> x1, Pallas kernels: none -> 43.4 us  [compact(): pl.pallas_call(functools.partial(kernel, n_rows, n_cols), out_shape=(jax....]
    psum x1 -> x0, waiting for transfers between devices: 37 us -> none  [local(): total_sum = lax.psum(quad_term, 'prow')]
    all_to_all x1 -> x0, waiting for transfers between devices: 36.9 us -> none  [local(): lax.all_to_all(z_rows, 'pcol', split_axis=1, concat_axis=1, tiled=True)]
    all_gather x1 -> x0, waiting for transfers between devices: 29.1 us -> none  [local(): rows_in = lax.all_gather(panel, 'prow', axis=2, tiled=True)]
    dot_general x28 -> x0, matrix products: 16.1 us -> none  [the longest x4 4.94 us: one_node(): jnp.einsum('sg,cigw->cisw', table_k, ainv_blocks, preferred_element_type=...]
    reduce_scatter x1 -> x0, waiting for transfers between devices: 11.5 us -> none  [local(): lax.psum_scatter(partial_value.reshape(2, rows_all, total_k * block_width...]
    reshape x3 -> x0, local copies, waits for them, and re-layouts: 7.57 us -> none  [the longest x1 4.76 us: local(): partial_value.reshape(2, rows_all, total_k * block_width)]
    dynamic_update_slice x4 -> x0, other arithmetic: 4.27 us -> none  [local(): per_node = lax.map(one_node, (pick_table, jnp.moveaxis(placed, 1, 0)))]
  transfers between devices with their start and end apart: 4 -> 0, of which waited for: 4 -> 0; matrix products, arithmetic and copies ran while one was open for 4% -> 0% of each run, Pallas kernels for 0% -> 0%
where the time goes in v1:
time: 51.8 us; the launch traced here: 51.5 us
  Pallas kernels  43.4 us (84%)
  local copies, waits for them, and re-layouts  4.75 us (9%)
  other arithmetic  2.02 us (4%)
  between operations  1.33 us (3%)
    pallas_call x1, Pallas kernels, compact(): pl.pallas_call(functools.partial(kernel, n_rows, n_cols), out_shape=(jax....  43.4 us
    unnamed x10, local copies, waits for them, and re-layouts  4.08 us
    select_n x1, other arithmetic, compact(): sel_inv = jnp.where(keep[None, :, None, None], -r[:, None], 0.0)  1.13 us

profile of v1, /device:TPU:0, one launch (start us, length us, event | category | flops | bytes accessed | tf_op | source)
XLA Modules:
  0.0 51.5 jit_solution(14808086033633688762)
XLA Ops:
  0.6 0.0 copy-start.3
  0.6 0.7 %copy-done.3 = s32[4,4]{1,0:T(4,128)S(1)} copy-done((s32[4,4]{1,0:T(4,128)S(1)}, s32[4,4]{1,0:T(4,128)}, u32[]{:S(2)}) %copy-start.3) | copy-done | bytes 88
  1.3 0.6 %dynamic_slice.3 = s32[1,1]{1,0:T(1,128)} dynamic-slice(s32[4,4]{1,0:T(4,128)S(1)} %copy-done.3, s32[]{:T(128)S(6)} %select_n.11, s32[]{:T(128)S(6)} %select_n.12), dynamic_slice_sizes={1,1} | dynamic-slice | bytes 12 | tf_op jit(solution)/shard_map/dynamic_slice | solution.py:267
  2.6 0.1 broadcast_in_dim.29
  2.7 0.0 copy-start
  2.7 1.2 %copy-done = bf16[2,512,512]{2,1,0:T(8,128)(2,1)S(1)} copy-done((bf16[2,512,512]{2,1,0:T(8,128)(2,1)S(1)}, bf16[2,512,512]{2,1,0:T(8,128)(2,1)}, u32[]{:S(2)}) %copy-start) | copy-done | bytes 1048600
  3.9 0.0 copy-start.1
  3.9 1.2 %copy-done.1 = bf16[2,4,256,256]{3,2,1,0:T(8,128)(2,1)S(1)} copy-done((bf16[2,4,256,256]{3,2,1,0:T(8,128)(2,1)S(1)}, bf16[2,4,256,256]{3,2,1,0:T(8,128)(2,1)}, u32[]{:S(2)}) %copy-start.1) | copy-done | bytes 1048600
  5.1 0.0 copy-start.2
  5.1 0.9 %copy-done.2 = bf16[2,4,64,256]{3,2,1,0:T(8,128)(2,1)S(1)} copy-done((bf16[2,4,64,256]{3,2,1,0:T(8,128)(2,1)S(1)}, bf16[2,4,64,256]{3,2,1,0:T(8,128)(2,1)}, u32[]{:S(2)}) %copy-start.2) | copy-done | bytes 262168
  6.1 43.4 %shard_map.68 = (f32[2,256,256]{2,1,0:T(8,128)S(1)}, bf16[2,256,256]{2,1,0:T(8,128)(2,1)S(1)}) custom-call(s32[4,4]{1,0:T(4,128)S(1)} %copy-done.3, bf16[2,512,512]{2,1,0:T(8,128)(2,1)S(1)} %copy-done, bf16[2,4,64,256]{3,2,1,0:T(8,128)(2,1)S(1)} %copy-done.2, bf16[2,4,256,256]{3,2,1,0:T(8,128)(2,1)S(1)} %copy-done.1), custom_call_target="tpu_custom_call" | custom-call | tf_op jit(solution)/shard_map/pallas_call | solution.py:230
  49.5 0.0 copy-start.4
  49.5 1.1 %bitcast_select_fusion = f32[2,512,256]{2,1,0:T(8,128)} fusion(f32[2,256,256]{2,1,0:T(8,128)S(1)} %neg.4, pred[512]{0:T(512)(128)(4,1)S(1)} %broadcast_in_dim.30), kind=kLoop, calls=%fused_computation | loop fusion | flops 262144 | bytes 1573376 | tf_op jit(solution)/shard_map/jit(_where)/select_n | solution.py:269
  50.7 0.0 copy-done.4
  50.7 0.9 %fusion = f32[2,1,256,256]{3,2,1,0:T(8,128)} fusion(f32[2,1,256,256]{3,2,1,0:T(8,128)S(1)} %copy-done.4, bf16[2,256,256]{2,1,0:T(8,128)(2,1)S(1)} %get-tuple-element.5), kind=kLoop, calls=%fused_computation.2 | loop fusion | flops 262144 | bytes 1310720
  (3 shorter events, 0.1 us)
Async XLA Ops:
  0.6 0.7 %copy-start.3 = (s32[4,4]{1,0:T(4,128)S(1)}, s32[4,4]{1,0:T(4,128)}, u32[]{:S(2)}) copy-start(s32[4,4]{1,0:T(4,128)} %table.1) | copy-start | bytes 196
  2.7 1.2 %copy-start = (bf16[2,512,512]{2,1,0:T(8,128)(2,1)S(1)}, bf16[2,512,512]{2,1,0:T(8,128)(2,1)}, u32[]{:S(2)}) copy-start(bf16[2,512,512]{2,1,0:T(8,128)(2,1)} %a_hbm.1) | copy-start | bytes 3145732
  3.9 1.2 %copy-start.1 = (bf16[2,4,256,256]{3,2,1,0:T(8,128)(2,1)S(1)}, bf16[2,4,256,256]{3,2,1,0:T(8,128)(2,1)}, u32[]{:S(2)}) copy-start(bf16[2,4,256,256]{3,2,1,0:T(8,128)(2,1)} %u_hbm.1) | copy-start | bytes 3145732
  5.1 0.9 %copy-start.2 = (bf16[2,4,64,256]{3,2,1,0:T(8,128)(2,1)S(1)}, bf16[2,4,64,256]{3,2,1,0:T(8,128)(2,1)}, u32[]{:S(2)}) copy-start(bf16[2,4,64,256]{3,2,1,0:T(8,128)(2,1)} %panel_hbm.1) | copy-start | bytes 786436
  49.5 1.1 %copy-start.4 = (f32[2,1,256,256]{3,2,1,0:T(8,128)S(1)}, f32[2,1,256,256]{3,2,1,0:T(8,128)}, u32[]{:S(2)}) copy-start(f32[2,1,256,256]{3,2,1,0:T(8,128)} %param.8) | copy-start | bytes 1572868

commit v2 on v1

--- a/solution.py
+++ b/solution.py
@@ -32,8 +32,8 @@
 
 
 def kernel(
-    n_rows, n_cols, table, a_hbm, panel_hbm, u_hbm, r_out, t_out,
-    av, pv, uv, pr, gather, pick_out, pick_in, acc, qsend_buf, qrecv_buf, tot,
+    n_rows, n_cols, table, a_hbm, panel_hbm, u_hbm, k_hbm, sel_out, diag_out,
+    av, pv, uv, pr, gather, pick_out, pick_in, acc, r_buf, sel_buf, kv, qsend_buf, qrecv_buf, tot,
     local_sem, p_send, p_recv, a_send, a_recv, g_send, g_recv, q_send, q_recv, t_send, t_recv,
 ):
     row = lax.axis_index("prow")
@@ -50,9 +50,11 @@
     copy_p = pltpu.make_async_copy(panel_hbm, pv, local_sem.at[0])
     copy_u = pltpu.make_async_copy(u_hbm.at[:, col], uv, local_sem.at[1])
     copy_a = pltpu.make_async_copy(a_hbm, av, local_sem.at[2])
+    copy_k = pltpu.make_async_copy(k_hbm, kv, local_sem.at[3])
     copy_p.start()
     copy_u.start()
     copy_a.start()
+    copy_k.start()
 
     barrier = pltpu.get_barrier_semaphore()
     for unit in range(1, n_cols):
@@ -124,29 +126,27 @@
         pick(unit)
         pick_copy(unit, col).start()
     pick(0)
-    for unit in range(2, n_cols):
-        scale(unit)
-
-    for unit in range(n_cols):
-        for step in range(1, n_rows):
-            below, above = row - step, row + step
-
-            @pl.when(below >= 0)
+
+    def forward(unit, step):
+        below, above = row - step, row + step
+
+        @pl.when(below >= 0)
+        def _():
+            line_copy(unit, below, step, 0).wait_recv()
+
+            @pl.when(row < n_rows - 1)
             def _():
-                line_copy(unit, below, step, 0).wait_recv()
-
-                @pl.when(row < n_rows - 1)
-                def _():
-                    line_copy(unit, below, step, 0).start()
-
-            @pl.when(above <= n_rows - 1)
+                line_copy(unit, below, step, 0).start()
+
+        @pl.when(above <= n_rows - 1)
+        def _():
+            line_copy(unit, above, step, 1).wait_recv()
+
+            @pl.when(row > 0)
             def _():
-                line_copy(unit, above, step, 1).wait_recv()
-
-                @pl.when(row > 0)
-                def _():
-                    line_copy(unit, above, step, 1).start()
-
+                line_copy(unit, above, step, 1).start()
+
+    def multiply(unit):
         slot = peer(unit)
         if unit == 0:
             left = (pick_out[0, 0], pick_out[0, 1])
@@ -162,12 +162,29 @@
             acc[0] += real
             acc[1] += imag
 
+    early, late = (0, 1), range(2, n_cols)
+    for unit in early:
+        forward(unit, 1)
+    for unit in late:
+        scale(unit)
+    for step in range(2, n_rows + 1):
+        for unit in early:
+            if step < n_rows:
+                forward(unit, step)
+        for unit in late:
+            forward(unit, step - 1)
+        if step == n_rows - 1:
+            for unit in early:
+                multiply(unit)
+    for unit in late:
+        multiply(unit)
+
     live = (jnp.full((1, width), table[col, row]) >= 0).astype(F32)
     unit_here = ((row // 2 - col // 2 + pairs) % pairs) * 2 + (row + col) % 2
     z = tuple(gather[unit_here, plane].reshape(width, width) for plane in range(2))
     r = (acc[0] * live, acc[1] * live)
-    r_out[0] = r[0]
-    r_out[1] = r[1]
+    r_buf[0] = r[0]
+    r_buf[1] = r[1]
     real, imag = cdot(z, (r[0].astype(BF16), r[1].astype(BF16)), (((0,), (0,)), ((), ())))
     acc[0] = real
     acc[1] = imag
@@ -184,6 +201,14 @@
 
     for step in range(1, n_rows):
         quad_copy(step, row).start()
+    named = jnp.full((1, width), table[col, row]) - row * row_blocks
+    for i in range(row_blocks):
+        keep = -(named == i).astype(F32)
+        for plane in range(2):
+            sel_buf[plane, i * width : (i + 1) * width, :] = r_buf[plane] * keep
+    copy_s = pltpu.make_async_copy(sel_buf, sel_out, local_sem.at[4])
+    copy_s.start()
+    copy_k.wait()
     mine = pl.ds(pl.multiple_of(row * part, part), part)
     sums = [acc[0, mine, :], acc[1, mine, :]]
     for step in range(1, n_rows):
@@ -198,8 +223,9 @@
     for step in range(1, n_rows):
         total_copy(step, (row + step) % n_rows).wait_recv()
     for plane in range(2):
-        t_out[plane] = tot[:, plane].reshape(width, width)
-
+        diag_out[plane, 0] = kv[plane, 0] + tot[:, plane].reshape(width, width).astype(F32)
+
+    copy_s.wait()
     for unit in range(1, n_cols):
         panel_copy(unit, col).wait_send()
         pick_copy(unit, col).wait_send()
@@ -224,17 +250,17 @@
     n_rows, n_cols = lax.axis_size("prow"), lax.axis_size("pcol")
     width, part = u_inv.shape[-1], panel.shape[2]
     row_blocks = ainv_anc.shape[1] // width
-    hbm = pl.BlockSpec(memory_space=pl.ANY)
+    hbm = pl.BlockSpec(memory_space=pltpu.HBM)
     vmem = pl.BlockSpec(memory_space=pltpu.VMEM)
     dma = pltpu.SemaphoreType.DMA
-    r, total = pl.pallas_call(
+    return pl.pallas_call(
         functools.partial(kernel, n_rows, n_cols),
         out_shape=(
-            jax.ShapeDtypeStruct((2, width, width), F32),
-            jax.ShapeDtypeStruct((2, width, width), BF16),
+            jax.ShapeDtypeStruct((2, row_blocks * width, width), F32),
+            jax.ShapeDtypeStruct(k_inv.shape, F32),
         ),
-        in_specs=[pl.BlockSpec(memory_space=pltpu.SMEM), hbm, hbm, hbm],
-        out_specs=(vmem, vmem),
+        in_specs=[pl.BlockSpec(memory_space=pltpu.SMEM), hbm, hbm, hbm, hbm],
+        out_specs=(hbm, vmem),
         scratch_shapes=[
             pltpu.VMEM(ainv_anc.shape, BF16),
             pltpu.VMEM(panel.shape, BF16),
@@ -244,10 +270,13 @@
             pltpu.VMEM((n_cols, 2, width, width), BF16),
             pltpu.VMEM((n_cols, 2, width, width), BF16),
             pltpu.VMEM((2, width, width), F32),
+            pltpu.VMEM((2, width, width), F32),
+            pltpu.VMEM((2, row_blocks * width, width), F32),
+            pltpu.VMEM(k_inv.shape, F32),
             pltpu.VMEM((n_rows, 2, part, width), BF16),
             pltpu.VMEM((n_rows, 2, part, width), BF16),
             pltpu.VMEM((n_rows, 2, part, width), BF16),
-            dma((3,)),
+            dma((5,)),
             dma((n_cols,)),
             dma((n_cols,)),
             dma((n_cols,)),
@@ -260,15 +289,9 @@
             dma((n_rows,)),
         ],
         compiler_params=pltpu.CompilerParams(
-            collective_id=0, has_side_effects=True, vmem_limit_bytes=24 * 1024 * 1024
+            collective_id=0, has_side_effects=True
         ),
-    )(structure, ainv_anc, panel, u_inv)
-    row, col = lax.axis_index("prow"), lax.axis_index("pcol")
-    named = structure[col, row] - row * row_blocks
-    keep = named == jnp.arange(row_blocks, dtype=jnp.int32)
-    sel_inv = jnp.where(keep[None, :, None, None], -r[:, None], 0.0)
-    diag_inv = k_inv + total[:, None].astype(F32)
-    return sel_inv.reshape(2, row_blocks * width, width), diag_inv
+    )(structure, ainv_anc, panel, u_inv, k_inv)
 
 
 def complex_quad(z_part, s_part):

time: 51.8 us -> 45.8 us (0.88)
  other arithmetic: 2.02 us -> 0 us
  local copies, waits for them, and re-layouts: 4.75 us -> 3.12 us
  Pallas kernels: 43.4 us -> 41.9 us
  between operations: 1.33 us -> 0.65 us
    pallas_call x1, Pallas kernels: 43.4 us -> 41.9 us  [compact(): pl.pallas_call(functools.partial(kernel, n_rows, n_cols), out_shape=(jax....]
    select_n x1 -> x0, other arithmetic: 1.13 us -> none  [compact(): sel_inv = jnp.where(keep[None, :, None, None], -r[:, None], 0.0)]
    unnamed x10 -> x4, local copies, waits for them, and re-layouts: 4.08 us -> 3.12 us
    unnamed x1 -> x0, other arithmetic: 0.85 us -> none
    dynamic_slice x1 -> x0, local copies, waits for them, and re-layouts: 0.58 us -> none  [compact(): named = structure[col, row] - row * row_blocks]
where the time goes in v2:
time: 45.8 us; the launch traced here: 45.6 us
  Pallas kernels  41.9 us (91%)
  local copies, waits for them, and re-layouts  3.12 us (7%)
  between operations  0.65 us (1%)
    pallas_call x1, Pallas kernels, compact(): pl.pallas_call(functools.partial(kernel, n_rows, n_cols), out_shape=(jax....  41.9 us
    unnamed x4, local copies, waits for them, and re-layouts  3.12 us

profile of v2, /device:TPU:0, one launch (start us, length us, event | category | flops | bytes accessed | tf_op | source)
XLA Modules:
  0.0 45.6 jit_solution(17135643708097335323)
XLA Ops:
  0.6 41.9 %shard_map.68 = (f32[2,512,256]{2,1,0:T(8,128)}, f32[2,1,256,256]{3,2,1,0:T(8,128)}) custom-call(s32[4,4]{1,0:T(4,128)} %table.1, bf16[2,512,512]{2,1,0:T(8,128)(2,1)} %a_hbm.1, bf16[2,4,64,256]{3,2,1,0:T(8,128)(2,1)} %panel_hbm.1, bf16[2,4,256,256]{3,2,1,0:T(8,128)(2,1)} %u_hbm.1, f32[2,1,256,256]{3,2,1,0:T(8,128)} %k_hbm.1), custom_call_target="tpu_custom_call" | custom-call | tf_op jit(solution)/shard_map/pallas_call | solution.py:256
  42.5 0.0 copy-start
  42.5 2.3 %copy.9 = f32[2,512,256]{2,1,0:T(8,128)} copy(f32[2,512,256]{2,1,0:T(8,128)} %get-tuple-element.4) | data formatting | bytes 2097152
  44.8 0.0 copy-done
  44.9 0.8 %copy.10 = f32[2,1,256,256]{3,2,1,0:T(8,128)} copy(f32[2,1,256,256]{3,2,1,0:T(8,128)S(1)} %copy-done) | data formatting | bytes 1048576
Async XLA Ops:
  42.5 2.3 %copy-start = (f32[2,1,256,256]{3,2,1,0:T(8,128)S(1)}, f32[2,1,256,256]{3,2,1,0:T(8,128)}, u32[]{:S(2)}) copy-start(f32[2,1,256,256]{3,2,1,0:T(8,128)} %get-tuple-element.5) | copy-start | bytes 1572868

commit v3 on v2

--- a/solution.py
+++ b/solution.py
@@ -59,11 +59,17 @@
     barrier = pltpu.get_barrier_semaphore()
     for unit in range(1, n_cols):
         pl.semaphore_signal(barrier, inc=1, device_id={"pcol": peer(unit)}, device_id_type=pl.DeviceIdType.MESH)
-    for step in range(1, n_rows):
-        pl.semaphore_signal(
-            barrier, inc=1, device_id={"prow": (row + step) % n_rows}, device_id_type=pl.DeviceIdType.MESH
-        )
-    pl.semaphore_wait(barrier, n_cols + n_rows - 2)
+
+    @pl.when(row > 0)
+    def _():
+        pl.semaphore_signal(barrier, inc=1, device_id={"prow": row - 1}, device_id_type=pl.DeviceIdType.MESH)
+
+    @pl.when(row < n_rows - 1)
+    def _():
+        pl.semaphore_signal(barrier, inc=1, device_id={"prow": row + 1}, device_id_type=pl.DeviceIdType.MESH)
+
+    ends = (row == 0).astype(jnp.int32) + (row == n_rows - 1).astype(jnp.int32)
+    pl.semaphore_wait(barrier, n_cols + 1 - ends)
 
     def panel_copy(unit, source):
         return remote(
@@ -173,34 +179,41 @@
                 forward(unit, step)
         for unit in late:
             forward(unit, step - 1)
+            if step == n_rows:
+                multiply(unit)
         if step == n_rows - 1:
             for unit in early:
                 multiply(unit)
-    for unit in late:
-        multiply(unit)
-
     live = (jnp.full((1, width), table[col, row]) >= 0).astype(F32)
     unit_here = ((row // 2 - col // 2 + pairs) % pairs) * 2 + (row + col) % 2
     z = tuple(gather[unit_here, plane].reshape(width, width) for plane in range(2))
     r = (acc[0] * live, acc[1] * live)
     r_buf[0] = r[0]
     r_buf[1] = r[1]
-    real, imag = cdot(z, (r[0].astype(BF16), r[1].astype(BF16)), (((0,), (0,)), ((), ())))
-    acc[0] = real
-    acc[1] = imag
-    for plane in range(2):
-        qsend_buf[:, plane] = acc[plane].reshape(n_rows, part, width).astype(BF16)
-
-    def quad_copy(step, source):
+    halves = 2
+    half_width = width // halves
+
+    def quad_copy(half, step, source):
         there = (row + step) % n_rows
-        return remote(qsend_buf.at[there], qrecv_buf.at[source], q_send.at[step], q_recv.at[source], {"prow": there})
-
-    def total_copy(step, source):
+        return remote(
+            qsend_buf.at[half, there], qrecv_buf.at[half, source],
+            q_send.at[half, step], q_recv.at[half, source], {"prow": there},
+        )
+
+    def total_copy(half, step, source):
         there = (row + step) % n_rows
-        return remote(tot.at[source], tot.at[source], t_send.at[step], t_recv.at[source], {"prow": there})
-
-    for step in range(1, n_rows):
-        quad_copy(step, row).start()
+        block = tot.at[half, source]
+        return remote(block, block, t_send.at[half, step], t_recv.at[half, source], {"prow": there})
+
+    low = (r[0].astype(BF16), r[1].astype(BF16))
+    for half in range(halves):
+        columns = slice(half * half_width, (half + 1) * half_width)
+        quad = cdot(z, (low[0][:, columns], low[1][:, columns]), (((0,), (0,)), ((), ())))
+        for plane in range(2):
+            acc[plane, :, columns] = quad[plane]
+            qsend_buf[half, :, plane] = quad[plane].reshape(n_rows, part, half_width).astype(BF16)
+        for step in range(1, n_rows):
+            quad_copy(half, step, row).start()
     named = jnp.full((1, width), table[col, row]) - row * row_blocks
     for i in range(row_blocks):
         keep = -(named == i).astype(F32)
@@ -210,20 +223,26 @@
     copy_s.start()
     copy_k.wait()
     mine = pl.ds(pl.multiple_of(row * part, part), part)
-    sums = [acc[0, mine, :], acc[1, mine, :]]
-    for step in range(1, n_rows):
-        source = (row + step) % n_rows
-        quad_copy(step, source).wait_recv()
+    for half in range(halves):
+        columns = slice(half * half_width, (half + 1) * half_width)
+        sums = [acc[0, mine, columns], acc[1, mine, columns]]
+        for step in range(1, n_rows):
+            source = (row + step) % n_rows
+            quad_copy(half, step, source).wait_recv()
+            for plane in range(2):
+                sums[plane] = sums[plane] + qrecv_buf[half, source, plane].astype(F32)
         for plane in range(2):
-            sums[plane] = sums[plane] + qrecv_buf[source, plane].astype(F32)
-    for plane in range(2):
-        tot[row, plane] = sums[plane].astype(BF16)
-    for step in range(1, n_rows):
-        total_copy(step, row).start()
-    for step in range(1, n_rows):
-        total_copy(step, (row + step) % n_rows).wait_recv()
-    for plane in range(2):
-        diag_out[plane, 0] = kv[plane, 0] + tot[:, plane].reshape(width, width).astype(F32)
+            tot[half, row, plane] = sums[plane].astype(BF16)
+        for step in range(1, n_rows):
+            total_copy(half, step, row).start()
+    for half in range(halves):
+        columns = slice(half * half_width, (half + 1) * half_width)
+        for step in range(1, n_rows):
+            total_copy(half, step, (row + step) % n_rows).wait_recv()
+        for plane in range(2):
+            diag_out[plane, 0, :, columns] = (
+                kv[plane, 0, :, columns] + tot[half, :, plane].reshape(width, half_width).astype(F32)
+            )
 
     copy_s.wait()
     for unit in range(1, n_cols):
@@ -242,8 +261,9 @@
                 line_copy(unit, above, step, 1).wait_send()
 
     for step in range(1, n_rows):
-        quad_copy(step, row).wait_send()
-        total_copy(step, row).wait_send()
+        for half in range(halves):
+            quad_copy(half, step, row).wait_send()
+            total_copy(half, step, row).wait_send()
 
 
 def compact(ainv_anc, panel, u_inv, k_inv, structure):
@@ -273,9 +293,9 @@
             pltpu.VMEM((2, width, width), F32),
             pltpu.VMEM((2, row_blocks * width, width), F32),
             pltpu.VMEM(k_inv.shape, F32),
-            pltpu.VMEM((n_rows, 2, part, width), BF16),
-            pltpu.VMEM((n_rows, 2, part, width), BF16),
-            pltpu.VMEM((n_rows, 2, part, width), BF16),
+            pltpu.VMEM((2, n_rows, 2, part, width // 2), BF16),
+            pltpu.VMEM((2, n_rows, 2, part, width // 2), BF16),
+            pltpu.VMEM((2, n_rows, 2, part, width // 2), BF16),
             dma((5,)),
             dma((n_cols,)),
             dma((n_cols,)),
@@ -283,10 +303,10 @@
             dma((n_cols,)),
             dma((n_cols, 2, n_rows)),
             dma((n_cols, n_rows)),
-            dma((n_rows,)),
-            dma((n_rows,)),
-            dma((n_rows,)),
-            dma((n_rows,)),
+            dma((2, n_rows)),
+            dma((2, n_rows)),
+            dma((2, n_rows)),
+            dma((2, n_rows)),
         ],
         compiler_params=pltpu.CompilerParams(
             collective_id=0, has_side_effects=True

time: 45.8 us -> 44.1 us (0.963)
  Pallas kernels: 41.9 us -> 40.1 us
    pallas_call x1, Pallas kernels: 41.9 us -> 40.1 us  [compact(): pl.pallas_call(functools.partial(kernel, n_rows, n_cols), out_shape=(jax....]
where the time goes in v3:
time: 44.1 us; the launch traced here: 43.9 us
  Pallas kernels  40.1 us (91%)
  local copies, waits for them, and re-layouts  3.12 us (7%)
  between operations  0.65 us (1%)
    pallas_call x1, Pallas kernels, compact(): pl.pallas_call(functools.partial(kernel, n_rows, n_cols), out_shape=(jax....  40.1 us
    unnamed x4, local copies, waits for them, and re-layouts  3.12 us

profile of v3, /device:TPU:0, one launch (start us, length us, event | category | flops | bytes accessed | tf_op | source)
XLA Modules:
  0.0 43.9 jit_solution(18278802115322248990)
XLA Ops:
  0.6 40.1 %shard_map.68 = (f32[2,512,256]{2,1,0:T(8,128)}, f32[2,1,256,256]{3,2,1,0:T(8,128)}) custom-call(s32[4,4]{1,0:T(4,128)} %table.1, bf16[2,512,512]{2,1,0:T(8,128)(2,1)} %a_hbm.1, bf16[2,4,64,256]{3,2,1,0:T(8,128)(2,1)} %panel_hbm.1, bf16[2,4,256,256]{3,2,1,0:T(8,128)(2,1)} %u_hbm.1, f32[2,1,256,256]{3,2,1,0:T(8,128)} %k_hbm.1), custom_call_target="tpu_custom_call" | custom-call | tf_op jit(solution)/shard_map/pallas_call | solution.py:276
  40.8 0.0 copy-start
  40.8 2.3 %copy.9 = f32[2,512,256]{2,1,0:T(8,128)} copy(f32[2,512,256]{2,1,0:T(8,128)} %get-tuple-element.4) | data formatting | bytes 2097152
  43.1 0.0 copy-done
  43.1 0.8 %copy.10 = f32[2,1,256,256]{3,2,1,0:T(8,128)} copy(f32[2,1,256,256]{3,2,1,0:T(8,128)S(1)} %copy-done) | data formatting | bytes 1048576
Async XLA Ops:
  40.8 2.3 %copy-start = (f32[2,1,256,256]{3,2,1,0:T(8,128)S(1)}, f32[2,1,256,256]{3,2,1,0:T(8,128)}, u32[]{:S(2)}) copy-start(f32[2,1,256,256]{3,2,1,0:T(8,128)} %get-tuple-element.5) | copy-start | bytes 1572868

commit v4 on v3

--- a/solution.py
+++ b/solution.py
@@ -34,7 +34,7 @@
 def kernel(
     n_rows, n_cols, table, a_hbm, panel_hbm, u_hbm, k_hbm, sel_out, diag_out,
     av, pv, uv, pr, gather, pick_out, pick_in, acc, r_buf, sel_buf, kv, qsend_buf, qrecv_buf, tot,
-    local_sem, p_send, p_recv, a_send, a_recv, g_send, g_recv, q_send, q_recv, t_send, t_recv,
+    local_sem, p_send, p_recv, a_send, a_recv, g_send, g_recv, q_send, q_recv, t_send, t_recv, f_send,
 ):
     row = lax.axis_index("prow")
     col = lax.axis_index("pcol")
@@ -53,8 +53,6 @@
     copy_k = pltpu.make_async_copy(k_hbm, kv, local_sem.at[3])
     copy_p.start()
     copy_u.start()
-    copy_a.start()
-    copy_k.start()
 
     barrier = pltpu.get_barrier_semaphore()
     for unit in range(1, n_cols):
@@ -87,6 +85,7 @@
         return remote(block, block, g_send.at[unit, side, step], g_recv.at[unit, chunk], {"prow": there})
 
     copy_p.wait()
+    copy_a.start()
     for unit in range(1, n_cols):
         panel_copy(unit, col).start()
     copy_u.wait()
@@ -127,6 +126,7 @@
     scale(0)
     scale(1)
     copy_a.wait()
+    copy_k.start()
     order = list(range(2, n_cols)) + [1]
     for unit in order:
         pick(unit)
@@ -190,20 +190,42 @@
     r = (acc[0] * live, acc[1] * live)
     r_buf[0] = r[0]
     r_buf[1] = r[1]
-    halves = 2
+    halves, pieces = 2, 2
     half_width = width // halves
 
-    def quad_copy(half, step, source):
+    def band(piece):
+        return pl.ds(piece * (part // pieces), part // pieces)
+
+    def quad_copy(half, piece, step, source):
         there = (row + step) % n_rows
         return remote(
-            qsend_buf.at[half, there], qrecv_buf.at[half, source],
-            q_send.at[half, step], q_recv.at[half, source], {"prow": there},
-        )
-
-    def total_copy(half, step, source):
-        there = (row + step) % n_rows
-        block = tot.at[half, source]
-        return remote(block, block, t_send.at[half, step], t_recv.at[half, source], {"prow": there})
+            qsend_buf.at[half, there, :, band(piece)], qrecv_buf.at[half, source, :, band(piece)],
+            q_send.at[half, piece, step], q_recv.at[half, piece, source], {"prow": there},
+        )
+
+    middle = n_rows // 2
+
+    def total_copy(half, piece, source, target, sem):
+        block = tot.at[half, source, :, band(piece)]
+        return remote(block, block, sem.at[half, piece, target], t_recv.at[half, piece, source], {"prow": target})
+
+    def direct(target):
+        if target in (middle - 1, middle):
+            return row != target
+        return (row != target) & ((row < middle) if target < middle else (row >= middle))
+
+    def gate(source):
+        return row == (middle if source < middle else middle - 1)
+
+    def pass_on(half, piece):
+        for source in range(n_rows):
+            outer = range(middle + 1, n_rows) if source < middle else range(middle - 1)
+
+            @pl.when(gate(source))
+            def _():
+                total_copy(half, piece, source, source, t_send).wait_recv()
+                for target in outer:
+                    total_copy(half, piece, source, target, f_send.at[source]).start()
 
     low = (r[0].astype(BF16), r[1].astype(BF16))
     for half in range(halves):
@@ -212,8 +234,9 @@
         for plane in range(2):
             acc[plane, :, columns] = quad[plane]
             qsend_buf[half, :, plane] = quad[plane].reshape(n_rows, part, half_width).astype(BF16)
-        for step in range(1, n_rows):
-            quad_copy(half, step, row).start()
+        for piece in range(pieces):
+            for step in range(1, n_rows):
+                quad_copy(half, piece, step, row).start()
     named = jnp.full((1, width), table[col, row]) - row * row_blocks
     for i in range(row_blocks):
         keep = -(named == i).astype(F32)
@@ -222,23 +245,40 @@
     copy_s = pltpu.make_async_copy(sel_buf, sel_out, local_sem.at[4])
     copy_s.start()
     copy_k.wait()
-    mine = pl.ds(pl.multiple_of(row * part, part), part)
+    rows_piece = part // pieces
+    order_here = []
     for half in range(halves):
         columns = slice(half * half_width, (half + 1) * half_width)
-        sums = [acc[0, mine, columns], acc[1, mine, columns]]
-        for step in range(1, n_rows):
-            source = (row + step) % n_rows
-            quad_copy(half, step, source).wait_recv()
+        for piece in range(pieces):
+            mine = pl.ds(pl.multiple_of(row * part + piece * rows_piece, rows_piece), rows_piece)
+            sums = [acc[0, mine, columns], acc[1, mine, columns]]
+            for step in range(1, n_rows):
+                source = (row + step) % n_rows
+                quad_copy(half, piece, step, source).wait_recv()
+                for plane in range(2):
+                    sums[plane] = sums[plane] + qrecv_buf[half, source, plane, band(piece)].astype(F32)
             for plane in range(2):
-                sums[plane] = sums[plane] + qrecv_buf[half, source, plane].astype(F32)
-        for plane in range(2):
-            tot[half, row, plane] = sums[plane].astype(BF16)
-        for step in range(1, n_rows):
-            total_copy(half, step, row).start()
+                tot[half, row, plane, band(piece)] = sums[plane].astype(BF16)
+            for target in range(n_rows):
+
+                @pl.when(direct(target))
+                def _():
+                    total_copy(half, piece, row, target, t_send).start()
+
+            order_here.append((half, piece))
+            if len(order_here) > 2:
+                pass_on(*order_here[-3])
+    for entry in order_here[-2:]:
+        pass_on(*entry)
     for half in range(halves):
         columns = slice(half * half_width, (half + 1) * half_width)
-        for step in range(1, n_rows):
-            total_copy(half, step, (row + step) % n_rows).wait_recv()
+        for source in range(n_rows):
+            for piece in range(pieces):
+
+                @pl.when((row != source) & jnp.logical_not(gate(source)))
+                def _():
+                    total_copy(half, piece, source, source, t_send).wait_recv()
+
         for plane in range(2):
             diag_out[plane, 0, :, columns] = (
                 kv[plane, 0, :, columns] + tot[half, :, plane].reshape(width, half_width).astype(F32)
@@ -262,8 +302,24 @@
 
     for step in range(1, n_rows):
         for half in range(halves):
-            quad_copy(half, step, row).wait_send()
-            total_copy(half, step, row).wait_send()
+            for piece in range(pieces):
+                quad_copy(half, piece, step, row).wait_send()
+
+    for half in range(halves):
+        for piece in range(pieces):
+            for target in range(n_rows):
+
+                @pl.when(direct(target))
+                def _():
+                    total_copy(half, piece, row, target, t_send).wait_send()
+
+            for source in range(n_rows):
+                outer = range(middle + 1, n_rows) if source < middle else range(middle - 1)
+
+                @pl.when(gate(source))
+                def _():
+                    for target in outer:
+                        total_copy(half, piece, source, target, f_send.at[source]).wait_send()
 
 
 def compact(ainv_anc, panel, u_inv, k_inv, structure):
@@ -303,10 +359,11 @@
             dma((n_cols,)),
             dma((n_cols, 2, n_rows)),
             dma((n_cols, n_rows)),
-            dma((2, n_rows)),
-            dma((2, n_rows)),
-            dma((2, n_rows)),
-            dma((2, n_rows)),
+            dma((2, 2, n_rows)),
+            dma((2, 2, n_rows)),
+            dma((2, 2, n_rows)),
+            dma((2, 2, n_rows)),
+            dma((n_rows, 2, 2, n_rows)),
         ],
         compiler_params=pltpu.CompilerParams(
             collective_id=0, has_side_effects=True

time: 44.1 us -> 46.3 us (1.050)
  Pallas kernels: 40.1 us -> 42.3 us
    pallas_call x1, Pallas kernels: 40.1 us -> 42.3 us  [compact(): pl.pallas_call(functools.partial(kernel, n_rows, n_cols), out_shape=(jax....]
where the time goes in v4:
time: 46.3 us; the launch traced here: 46.1 us
  Pallas kernels  42.3 us (91%)
  local copies, waits for them, and re-layouts  3.12 us (7%)
  between operations  0.65 us (1%)
    pallas_call x1, Pallas kernels, compact(): pl.pallas_call(functools.partial(kernel, n_rows, n_cols), out_shape=(jax....  42.3 us
    unnamed x4, local copies, waits for them, and re-layouts  3.12 us

profile of v4, /device:TPU:0, one launch (start us, length us, event | category | flops | bytes accessed | tf_op | source)
XLA Modules:
  0.0 46.1 jit_solution(4498600534922080312)
XLA Ops:
  0.6 42.3 %shard_map.68 = (f32[2,512,256]{2,1,0:T(8,128)}, f32[2,1,256,256]{3,2,1,0:T(8,128)}) custom-call(s32[4,4]{1,0:T(4,128)} %table.1, bf16[2,512,512]{2,1,0:T(8,128)(2,1)} %a_hbm.1, bf16[2,4,64,256]{3,2,1,0:T(8,128)(2,1)} %panel_hbm.1, bf16[2,4,256,256]{3,2,1,0:T(8,128)(2,1)} %u_hbm.1, f32[2,1,256,256]{3,2,1,0:T(8,128)} %k_hbm.1), custom_call_target="tpu_custom_call" | custom-call | tf_op jit(solution)/shard_map/pallas_call | solution.py:332
  43.0 0.0 copy-start
  43.0 2.3 %copy.9 = f32[2,512,256]{2,1,0:T(8,128)} copy(f32[2,512,256]{2,1,0:T(8,128)} %get-tuple-element.4) | data formatting | bytes 2097152
  45.3 0.0 copy-done
  45.3 0.8 %copy.10 = f32[2,1,256,256]{3,2,1,0:T(8,128)} copy(f32[2,1,256,256]{3,2,1,0:T(8,128)S(1)} %copy-done) | data formatting | bytes 1048576
Async XLA Ops:
  43.0 2.3 %copy-start = (f32[2,1,256,256]{3,2,1,0:T(8,128)S(1)}, f32[2,1,256,256]{3,2,1,0:T(8,128)}, u32[]{:S(2)}) copy-start(f32[2,1,256,256]{3,2,1,0:T(8,128)} %get-tuple-element.5) | copy-start | bytes 1572868

commit v5 on v4

--- a/solution.py
+++ b/solution.py
@@ -34,7 +34,7 @@
 def kernel(
     n_rows, n_cols, table, a_hbm, panel_hbm, u_hbm, k_hbm, sel_out, diag_out,
     av, pv, uv, pr, gather, pick_out, pick_in, acc, r_buf, sel_buf, kv, qsend_buf, qrecv_buf, tot,
-    local_sem, p_send, p_recv, a_send, a_recv, g_send, g_recv, q_send, q_recv, t_send, t_recv, f_send,
+    local_sem, p_send, p_recv, a_send, a_recv, g_send, g_recv, q_send, q_recv, t_send, t_recv,
 ):
     row = lax.axis_index("prow")
     col = lax.axis_index("pcol")
@@ -193,6 +193,12 @@
     halves, pieces = 2, 2
     half_width = width // halves
 
+    def diag_copy(half):
+        columns = pl.ds(half * half_width, half_width)
+        return pltpu.make_async_copy(
+            kv.at[:, :, :, columns], diag_out.at[:, :, :, columns], local_sem.at[5 + half]
+        )
+
     def band(piece):
         return pl.ds(piece * (part // pieces), part // pieces)
 
@@ -203,29 +209,10 @@
             q_send.at[half, piece, step], q_recv.at[half, piece, source], {"prow": there},
         )
 
-    middle = n_rows // 2
-
-    def total_copy(half, piece, source, target, sem):
+    def total_copy(half, piece, step, source):
+        there = (row + step) % n_rows
         block = tot.at[half, source, :, band(piece)]
-        return remote(block, block, sem.at[half, piece, target], t_recv.at[half, piece, source], {"prow": target})
-
-    def direct(target):
-        if target in (middle - 1, middle):
-            return row != target
-        return (row != target) & ((row < middle) if target < middle else (row >= middle))
-
-    def gate(source):
-        return row == (middle if source < middle else middle - 1)
-
-    def pass_on(half, piece):
-        for source in range(n_rows):
-            outer = range(middle + 1, n_rows) if source < middle else range(middle - 1)
-
-            @pl.when(gate(source))
-            def _():
-                total_copy(half, piece, source, source, t_send).wait_recv()
-                for target in outer:
-                    total_copy(half, piece, source, target, f_send.at[source]).start()
+        return remote(block, block, t_send.at[half, piece, step], t_recv.at[half, piece, source], {"prow": there})
 
     low = (r[0].astype(BF16), r[1].astype(BF16))
     for half in range(halves):
@@ -246,7 +233,6 @@
     copy_s.start()
     copy_k.wait()
     rows_piece = part // pieces
-    order_here = []
     for half in range(halves):
         columns = slice(half * half_width, (half + 1) * half_width)
         for piece in range(pieces):
@@ -259,32 +245,22 @@
                     sums[plane] = sums[plane] + qrecv_buf[half, source, plane, band(piece)].astype(F32)
             for plane in range(2):
                 tot[half, row, plane, band(piece)] = sums[plane].astype(BF16)
-            for target in range(n_rows):
-
-                @pl.when(direct(target))
-                def _():
-                    total_copy(half, piece, row, target, t_send).start()
-
-            order_here.append((half, piece))
-            if len(order_here) > 2:
-                pass_on(*order_here[-3])
-    for entry in order_here[-2:]:
-        pass_on(*entry)
+            for step in range(1, n_rows):
+                total_copy(half, piece, step, row).start()
     for half in range(halves):
         columns = slice(half * half_width, (half + 1) * half_width)
-        for source in range(n_rows):
+        for step in range(1, n_rows):
             for piece in range(pieces):
-
-                @pl.when((row != source) & jnp.logical_not(gate(source)))
-                def _():
-                    total_copy(half, piece, source, source, t_send).wait_recv()
-
+                total_copy(half, piece, step, (row + step) % n_rows).wait_recv()
         for plane in range(2):
-            diag_out[plane, 0, :, columns] = (
+            kv[plane, 0, :, columns] = (
                 kv[plane, 0, :, columns] + tot[half, :, plane].reshape(width, half_width).astype(F32)
             )
 
+        diag_copy(half).start()
     copy_s.wait()
+    for half in range(halves):
+        diag_copy(half).wait()
     for unit in range(1, n_cols):
         panel_copy(unit, col).wait_send()
         pick_copy(unit, col).wait_send()
@@ -304,22 +280,28 @@
         for half in range(halves):
             for piece in range(pieces):
                 quad_copy(half, piece, step, row).wait_send()
-
-    for half in range(halves):
-        for piece in range(pieces):
-            for target in range(n_rows):
-
-                @pl.when(direct(target))
-                def _():
-                    total_copy(half, piece, row, target, t_send).wait_send()
-
-            for source in range(n_rows):
-                outer = range(middle + 1, n_rows) if source < middle else range(middle - 1)
-
-                @pl.when(gate(source))
-                def _():
-                    for target in outer:
-                        total_copy(half, piece, source, target, f_send.at[source]).wait_send()
+                total_copy(half, piece, step, row).wait_send()
+
+
+def place(cuts, sel_hbm, diag_hbm, sel_out, diag_out, sel_buf, diag_buf, in_sem, out_sem):
+    rows = sel_hbm.shape[1] // cuts
+    ins, outs = [], []
+    for plane in range(2):
+        for cut in range(cuts):
+            at = (plane, pl.ds(cut * rows, rows))
+            index = plane * (cuts + 1) + cut
+            ins.append(pltpu.make_async_copy(sel_hbm.at[at], sel_buf.at[at], in_sem.at[index]))
+            outs.append(pltpu.make_async_copy(sel_buf.at[at], sel_out.at[at], out_sem.at[index]))
+        index = plane * (cuts + 1) + cuts
+        ins.append(pltpu.make_async_copy(diag_hbm.at[plane], diag_buf.at[plane], in_sem.at[index]))
+        outs.append(pltpu.make_async_copy(diag_buf.at[plane], diag_out.at[plane], out_sem.at[index]))
+    for copy in ins:
+        copy.start()
+    for load, store in zip(ins, outs):
+        load.wait()
+        store.start()
+    for copy in outs:
+        copy.wait()
 
 
 def compact(ainv_anc, panel, u_inv, k_inv, structure):
@@ -329,14 +311,15 @@
     hbm = pl.BlockSpec(memory_space=pltpu.HBM)
     vmem = pl.BlockSpec(memory_space=pltpu.VMEM)
     dma = pltpu.SemaphoreType.DMA
-    return pl.pallas_call(
+    shapes = (
+        jax.ShapeDtypeStruct((2, row_blocks * width, width), F32),
+        jax.ShapeDtypeStruct(k_inv.shape, F32),
+    )
+    results = pl.pallas_call(
         functools.partial(kernel, n_rows, n_cols),
-        out_shape=(
-            jax.ShapeDtypeStruct((2, row_blocks * width, width), F32),
-            jax.ShapeDtypeStruct(k_inv.shape, F32),
-        ),
+        out_shape=shapes,
         in_specs=[pl.BlockSpec(memory_space=pltpu.SMEM), hbm, hbm, hbm, hbm],
-        out_specs=(hbm, vmem),
+        out_specs=(hbm, hbm),
         scratch_shapes=[
             pltpu.VMEM(ainv_anc.shape, BF16),
             pltpu.VMEM(panel.shape, BF16),
@@ -352,7 +335,7 @@
             pltpu.VMEM((2, n_rows, 2, part, width // 2), BF16),
             pltpu.VMEM((2, n_rows, 2, part, width // 2), BF16),
             pltpu.VMEM((2, n_rows, 2, part, width // 2), BF16),
-            dma((5,)),
+            dma((7,)),
             dma((n_cols,)),
             dma((n_cols,)),
             dma((n_cols,)),
@@ -363,12 +346,24 @@
             dma((2, 2, n_rows)),
             dma((2, 2, n_rows)),
             dma((2, 2, n_rows)),
-            dma((n_rows, 2, 2, n_rows)),
         ],
         compiler_params=pltpu.CompilerParams(
             collective_id=0, has_side_effects=True
         ),
     )(structure, ainv_anc, panel, u_inv, k_inv)
+    cuts = 2
+    return pl.pallas_call(
+        functools.partial(place, cuts),
+        out_shape=shapes,
+        in_specs=[hbm, hbm],
+        out_specs=(hbm, hbm),
+        scratch_shapes=[
+            pltpu.VMEM(shapes[0].shape, F32),
+            pltpu.VMEM(shapes[1].shape, F32),
+            dma((2 * (cuts + 1),)),
+            dma((2 * (cuts + 1),)),
+        ],
+    )(*results)
 
 
 def complex_quad(z_part, s_part):

time: 46.3 us -> 43 us (0.929)
  local copies, waits for them, and re-layouts: 3.12 us -> 0 us
    unnamed x4 -> x0, local copies, waits for them, and re-layouts: 3.12 us -> none
    pallas_call x1 -> x2, Pallas kernels: 42.3 us -> 42.1 us  [the longest x1 40 us: compact(): pl.pallas_call(functools.partial(kernel, n_rows, n_cols), out_shape=shape...]
where the time goes in v5:
time: 43 us; the launch traced here: 42.8 us
  Pallas kernels  42.1 us (98%)
  between operations  0.64 us (1%)
    pallas_call x1, Pallas kernels, compact(): pl.pallas_call(functools.partial(kernel, n_rows, n_cols), out_shape=shape...  40 us
    pallas_call x1, Pallas kernels, compact(): pl.pallas_call(functools.partial(place, cuts), out_shape=shapes, in_specs...  2.19 us

profile of v5, /device:TPU:0, one launch (start us, length us, event | category | flops | bytes accessed | tf_op | source)
XLA Modules:
  0.0 42.8 jit_solution(9406063896892546508)
XLA Ops:
  0.6 40.0 %shard_map.68 = (f32[2,512,256]{2,1,0:T(8,128)}, f32[2,1,256,256]{3,2,1,0:T(8,128)}) custom-call(s32[4,4]{1,0:T(4,128)} %table.1, bf16[2,512,512]{2,1,0:T(8,128)(2,1)} %a_hbm.1, bf16[2,4,64,256]{3,2,1,0:T(8,128)(2,1)} %panel_hbm.1, bf16[2,4,256,256]{3,2,1,0:T(8,128)(2,1)} %u_hbm.1, f32[2,1,256,256]{3,2,1,0:T(8,128)} %k_hbm.1), custom_call_target="tpu_custom_call" | custom-call | tf_op jit(solution)/shard_map/pallas_call | solution.py:318
  40.6 2.2 %shard_map.69 = (f32[2,512,256]{2,1,0:T(8,128)}, f32[2,1,256,256]{3,2,1,0:T(8,128)}) custom-call(f32[2,512,256]{2,1,0:T(8,128)} %get-tuple-element.4.sel_hbm, f32[2,1,256,256]{3,2,1,0:T(8,128)} %get-tuple-element.5.diag_hbm), custom_call_target="tpu_custom_call" | custom-call | tf_op jit(solution)/shard_map/pallas_call | solution.py:355
